TPU v7x, 32 devices: a whole 2x2x4 slice. The times are simulated.
32 devices in a mesh: gx: 4 (over y, core), gy: 4 (over z), gz: 2 (over x).
Axes of the slice: x: 2, y: 2, z: 4, core: 2. Of those that a mesh axis runs over, the one named last changes fastest.
Arguments:
- fractions: float32 [3, 4, 8, 4, 128], P(None, 'gx', 'gy', 'gz'), may hold values from 0 to 1
- polarizability: float32 [4, 8, 4, 128], P('gx', 'gy', 'gz'), may hold values from 0.5 to 2
- occupancy: int32 [4, 8, 4, 128], P('gx', 'gy', 'gz'), may hold values 0 or 1
- pair_mask: int32 [4, 8, 4, 27], P('gx', 'gy', 'gz'), may hold values from 0 to 1, as said below
- perm_field: float32 [6, 4, 8, 4, 128], P(None, 'gx', 'gy', 'gz'), may hold values from -6 to 6
- history: float32 [6, 6, 4, 8, 4, 128], P(None, None, 'gx', 'gy', 'gz'), may hold values from -12 to 12
Outputs:
- induced: float32 [6, 4, 8, 4, 128], P(None, 'gx', 'gy', 'gz')
- change: float32 [], replicated
Inputs may be any that keep to these rules, and one draw needn't show every extreme that they name: pair_mask[t, k] equals pair_mask at tile t + offset(k) for the opposite offset 26 - k (periodic); pair_mask[t, 13] (the tile itself) is 1.
All inputs are finite; a program needn't handle non-finite values. No bound on the sum of `occupancy` on one device may be relied on, other than what follows from the above.
Results may differ from a plain program's by a relative error of at most 0.0003.
Values sent between devices are 32-bit elements; how exact they have to be, the bound alone decides.
A program may use at most 64 MiB of HBM per device.

v0:
```python
import jax
import jax.numpy as jnp
from jax import lax
from jax.sharding import PartitionSpec as P

CELL_EDGE = 10.0
SOFTENING = 0.3
THOLE_DAMP = 0.39
RELAXATION = 0.7


def with_halo(cells, sides, width):
    for axis, dim in sides:
        count = lax.axis_size(axis)
        head = lax.slice_in_dim(cells, 0, width, axis=dim)
        tail = lax.slice_in_dim(cells, cells.shape[dim] - width, cells.shape[dim], axis=dim)
        cells = jnp.concatenate(
            [
                lax.ppermute(tail, axis, [(i, (i + 1) % count) for i in range(count)]),
                cells,
                lax.ppermute(head, axis, [((i + 1) % count, i) for i in range(count)]),
            ],
            axis=dim,
        )
    return cells


def pair_field(target, source, moment, offset_vec, itself, allowed):
    displace = [
        (offset_vec[axis_num] + source[axis_num][:, None, :] - target[axis_num][:, :, None])
        * CELL_EDGE
        for axis_num in range(3)
    ]
    dist_sq = (
        displace[0] * displace[0]
        + displace[1] * displace[1]
        + displace[2] * displace[2]
        + SOFTENING
    )
    inv_cube = lax.rsqrt(dist_sq) / dist_sq
    thole_arg = (
        dist_sq * jnp.sqrt(dist_sq) * lax.rsqrt(target[3][:, :, None] * source[3][:, None, :])
    )
    damping = jnp.exp(-THOLE_DAMP * thole_arg)
    lambda_three = 1.0 - damping
    lambda_five = 1.0 - (1.0 + THOLE_DAMP * thole_arg) * damping
    slots = target.shape[-1]
    self_pair = jnp.logical_and(itself, jnp.eye(slots, dtype=bool))
    weight = jnp.where(self_pair, 0.0, allowed[:, None, None])
    radial = 3.0 * lambda_five * inv_cube / dist_sq * weight
    direct = lambda_three * inv_cube * weight
    fields = []
    for which_set in range(moment.shape[0] // 3):
        parts = [moment[3 * which_set + axis_num][:, None, :] for axis_num in range(3)]
        project = displace[0] * parts[0] + displace[1] * parts[1] + displace[2] * parts[2]
        for axis_num in range(3):
            fields.append(
                jnp.sum(radial * project * displace[axis_num] - direct * parts[axis_num], axis=-1)
            )
    return jnp.stack(fields)


def slab_field(geometry_pad, moment_pad, allowed_slab, slab_index):
    width_y = geometry_pad.shape[2] - 2
    width_z = geometry_pad.shape[3] - 2
    slots = geometry_pad.shape[4]
    rows = moment_pad.shape[0]
    zero = jnp.zeros((), jnp.int32)
    one = jnp.ones((), jnp.int32)
    first_x = (jnp.asarray(slab_index) + 1).astype(jnp.int32)
    target = lax.dynamic_slice(
        geometry_pad, (zero, first_x, one, one, zero), (4, 1, width_y, width_z, slots)
    ).reshape(4, width_y * width_z, slots)

    def offset_step(offset, summed):
        offset = jnp.asarray(offset).astype(jnp.int32)
        along_x = offset // 9 - 1
        along_y = offset // 3 % 3 - 1
        along_z = offset % 3 - 1
        starts = (zero, first_x + along_x, one + along_y, one + along_z, zero)
        source = lax.dynamic_slice(geometry_pad, starts, (4, 1, width_y, width_z, slots)).reshape(
            4, width_y * width_z, slots
        )
        moment = lax.dynamic_slice(moment_pad, starts, (rows, 1, width_y, width_z, slots)).reshape(
            rows, width_y * width_z, slots
        )
        allowed = (
            lax.dynamic_index_in_dim(allowed_slab, offset, 2, keepdims=False)
            .reshape(-1)
            .astype(jnp.float32)
        )
        offset_vec = jnp.stack([along_x, along_y, along_z]).astype(jnp.float32)
        return summed + pair_field(target, source, moment, offset_vec, offset == 13, allowed)

    summed = lax.fori_loop(
        0, 27, offset_step, jnp.zeros((rows, width_y * width_z, slots), jnp.float32)
    )
    return summed.reshape(rows, width_y, width_z, slots)


def device_field(geometry_pad, moment_pad, pair_mask):
    slabs = [slab_field(geometry_pad, moment_pad, pair_mask[0], 0)]
    return jnp.stack(slabs, 1)


def share_dipoles(dipoles):
    return with_halo(dipoles, (("gx", 1), ("gy", 2), ("gz", 3)), 1)


def global_gram(local_gram):
    return lax.psum(local_gram, ("gx", "gy", "gz"))


def fit_coefficients(gram_matrix):
    past_count = gram_matrix.shape[0] - 1
    gram_past = gram_matrix[:past_count, :past_count]
    gram_next = gram_matrix[:past_count, past_count]
    ridge_term = 0.001 * jnp.trace(gram_past) / past_count + 1.0
    factor = jnp.linalg.cholesky(gram_past + ridge_term * jnp.eye(past_count, dtype=jnp.float32))
    return jax.scipy.linalg.cho_solve((factor, True), gram_next)


def on_device(fractions, polarizability, occupancy, pair_mask, perm_field, history):
    filled = occupancy.astype(jnp.float32)
    geometry = jnp.concatenate([fractions, polarizability[None]], 0)
    masked = history * filled
    past_sets = masked.shape[0]
    flat_hist = masked.reshape(past_sets, -1)
    local_gram = jnp.dot(flat_hist, flat_hist.T, precision=lax.Precision.HIGHEST)
    scaled = RELAXATION * filled * polarizability
    later = masked[1:]
    coeffs = fit_coefficients(global_gram(local_gram))
    geometry_pad = with_halo(geometry, (("gx", 1), ("gy", 2), ("gz", 3)), 1)
    predicted = jnp.tensordot(coeffs, later, axes=1, precision=lax.Precision.HIGHEST)
    field_one = device_field(geometry_pad, share_dipoles(predicted), pair_mask)
    dipole_one = (1.0 - RELAXATION) * predicted + scaled * (perm_field + field_one)
    field_two = device_field(geometry_pad, share_dipoles(dipole_one), pair_mask)
    induced = (1.0 - RELAXATION) * dipole_one + scaled * (perm_field + field_two)
    update = induced - dipole_one
    totals = lax.psum((jnp.sum(update * update), jnp.sum(induced * induced)), ("gx", "gy", "gz"))
    change = jnp.sqrt(totals[0] / (totals[1] + 1.0))
    return (induced, change)


def solution(mesh):
    in_specs = (
        P(None, "gx", "gy", "gz", None),
        P("gx", "gy", "gz", None),
        P("gx", "gy", "gz", None),
        P("gx", "gy", "gz", None),
        P(None, "gx", "gy", "gz", None),
        P(None, None, "gx", "gy", "gz", None),
    )
    out_specs = (P(None, "gx", "gy", "gz", None), P())
    return jax.shard_map(
        on_device, mesh=mesh, in_specs=in_specs, out_specs=out_specs, check_vma=False
    )
```

profile of v0, /device:TPU:12, one launch (start us, length us, event | category | flops | bytes accessed | tf_op | source)
XLA Modules:
  0.0 395.9 jit_solution(7175893039068339655)
XLA Ops:
  3.1 41.2 %psum.21 = f32[6,6]{0,1:T(8,128)S(1)} all-reduce(f32[6,6]{0,1:T(8,128)S(1)} %convolution_bitcast_fusion), channel_id=1, replica_groups=mesh['gx'=4,'gy'=4,'gz'=2] {'gx','gy','gz'}, use_global_device_ids=true, to_apply=%region_0.0 | all-reduce | flops 36 | bytes 288 | tf_op jit(solution)/shard_map/psum | solution.py:111
  66.1 134.4 %while.38 = (s32[]{:T(128)}, f32[6,4,128]{2,1,0:T(4,128)S(1)}, f32[4,3,4,4,128]{4,3,2,1,0:T(4,128)S(1)}, f32[4,4,128]{2,1,0:T(4,128)S(1)}, s32[2,2,27]{1,0,2:T(2...) while((s32[]{:T(128)}, f32[6,4,128]{2,1,0:T(4,128)S(1)}, ...), condition=%wide.region_11.12_spmd.clone, body=%wide.region_4.11_spmd.clone.sunk | while | flops 6200888 | bytes 287493 | solution.py:95
  71.9 1.9 dynamic-slice_add_fusion.4
  76.9 1.9 dynamic-slice_add_fusion.4
  86.9 1.9 dynamic-slice_add_fusion.4
  91.9 1.9 dynamic-slice_add_fusion.4
  96.8 1.9 dynamic-slice_add_fusion.4
  106.8 1.9 dynamic-slice_add_fusion.4
  111.8 1.9 dynamic-slice_add_fusion.4
  116.7 1.9 dynamic-slice_add_fusion.4
  126.7 1.9 dynamic-slice_add_fusion.4
  131.7 1.9 dynamic-slice_add_fusion.4
  136.7 1.9 dynamic-slice_add_fusion.4
  146.6 1.9 dynamic-slice_add_fusion.4
  151.6 1.9 dynamic-slice_add_fusion.4
  166.5 1.9 dynamic-slice_add_fusion.4
  203.8 2.3 collective-permute-start.14
  208.6 2.6 collective-permute-done.15
  213.4 2.1 collective-permute-done.16
  216.8 133.6 %while.39 = (s32[]{:T(128)}, f32[6,4,128]{2,1,0:T(4,128)S(1)}, f32[4,3,4,4,128]{4,3,2,1,0:T(4,128)S(1)}, f32[4,4,128]{2,1,0:T(4,128)S(1)}, s32[2,2,27]{1,0,2:T(2...) while((s32[]{:T(128)}, f32[6,4,128]{2,1,0:T(4,128)S(1)}, ...), condition=%wide.region_19.20_spmd.clone, body=%wide.region_12.19_spmd.clone.sunk | while | flops 6200890 | bytes 262953 | solution.py:95
  217.7 1.9 constant_dynamic-slice_fusion.14
  222.6 1.9 constant_dynamic-slice_fusion.14
  227.5 1.9 constant_dynamic-slice_fusion.14
  232.5 1.9 constant_dynamic-slice_fusion.14
  237.4 1.9 constant_dynamic-slice_fusion.14
  242.4 1.9 constant_dynamic-slice_fusion.14
  247.3 1.9 constant_dynamic-slice_fusion.14
  252.3 1.9 constant_dynamic-slice_fusion.14
  257.2 1.9 constant_dynamic-slice_fusion.14
  262.2 1.9 constant_dynamic-slice_fusion.14
  267.1 1.9 constant_dynamic-slice_fusion.14
  272.1 1.9 constant_dynamic-slice_fusion.14
  277.0 1.9 constant_dynamic-slice_fusion.14
  282.0 1.9 constant_dynamic-slice_fusion.14
  286.9 1.9 constant_dynamic-slice_fusion.14
  291.9 1.9 constant_dynamic-slice_fusion.14
  296.8 1.9 constant_dynamic-slice_fusion.14
  301.8 1.9 constant_dynamic-slice_fusion.14
  306.7 1.9 constant_dynamic-slice_fusion.14
  311.7 1.9 constant_dynamic-slice_fusion.14
  316.6 1.9 constant_dynamic-slice_fusion.14
  321.6 1.9 constant_dynamic-slice_fusion.14
  326.5 1.9 constant_dynamic-slice_fusion.14
  331.5 1.9 constant_dynamic-slice_fusion.14
  336.4 1.9 constant_dynamic-slice_fusion.14
  341.4 1.9 constant_dynamic-slice_fusion.14
  346.3 1.9 constant_dynamic-slice_fusion.14
  351.8 41.8 %all-reduce = (f32[]{:T(128)}, f32[]{:T(128)}) all-reduce(f32[]{:T(128)} %get-tuple-element.589, f32[]{:T(128)} %get-tuple-element.588), channel_id=1, replica_groups=mesh['gx'=4,'gy'=4,'gz'=2] {'gx','gy','gz'}, use_global_device_ids=true, to_apply=%region_21.22 | all-reduce | flops 2 | bytes 16 | tf_op jit(solution)/shard_map/psum | solution.py:140
  (1234 shorter events, 212.3 us)
Async XLA Ops:
  2.2 0.9 copy-start
  48.5 2.1 copy-start.1
  48.7 1.8 copy-start.2
  48.7 7.1 %collective-permute-start.6 = (f32[6,1,2,2,128]{4,3,2,0,1:T(2,128)S(1)}, f32[6,1,2,2,128]{4,3,2,0,1:T(2,128)S(1)}, u32[]{:S(2)}, u32[]{:S(2)}) collective-permute-start(f32[6,1,2,2,128]{4,3,2,0,1:T(2,128)S(1)} %bitcast.219), channel_id=1, source_target_pairs={{0,8},{8,16},{16,24},{24,0},{1,9},{9,17},{17,25},{25,1},{2,10},{10... | collective-permute-start | bytes 36872 | tf_op jit(solution)/shard_map/ppermute | solution.py:19
  48.8 7.0 %collective-permute-start.7 = (f32[6,1,2,2,128]{4,3,2,0,1:T(2,128)S(1)}, f32[6,1,2,2,128]{4,3,2,0,1:T(2,128)S(1)}, u32[]{:S(2)}, u32[]{:S(2)}) collective-permute-start(f32[6,1,2,2,128]{4,3,2,0,1:T(2,128)S(1)} %bitcast.220), channel_id=1, source_target_pairs={{8,0},{16,8},{24,16},{0,24},{9,1},{17,9},{25,17},{1,25},{10,2},{18... | collective-permute-start | bytes 36872 | tf_op jit(solution)/shard_map/ppermute | solution.py:21
  50.5 1.8 copy-start.4
  50.6 3.2 collective-permute-start
  50.6 3.1 collective-permute-start.1
  52.4 0.7 copy-start.5
  53.8 4.6 %collective-permute-start.2 = (f32[4,3,1,2,128]{4,3,2,1,0:T(2,128)S(1)}, f32[4,3,1,2,128]{4,3,2,1,0:T(2,128)S(1)}, u32[]{:S(2)}, u32[]{:S(2)}) collective-permute-start(f32[4,3,1,2,128]{4,3,2,1,0:T(2,128)S(1)} %get-tuple-element.669), channel_id=1, source_target_pairs={{0,2},{2,4},{4,6},{6,0},{1,3},{3,5},{5,7},{7,1},{8,10},{10,12},{12... | collective-permute-start | bytes 36872 | tf_op jit(solution)/shard_map/ppermute | solution.py:19
  55.2 3.7 collective-permute-start.3
  55.9 5.2 %collective-permute-start.8 = (f32[6,3,1,2,128]{4,3,2,0,1:T(2,128)S(1)}, f32[6,3,1,2,128]{4,3,2,0,1:T(2,128)S(1)}, u32[]{:S(2)}, u32[]{:S(2)}) collective-permute-start(f32[6,3,1,2,128]{4,3,2,0,1:T(2,128)S(1)} %get-tuple-element.667), channel_id=1, source_target_pairs={{0,2},{2,4},{4,6},{6,0},{1,3},{3,5},{5,7},{7,1},{8,10},{10,12},{12... | collective-permute-start | bytes 55304 | tf_op jit(solution)/shard_map/ppermute | solution.py:19
  57.3 3.8 collective-permute-start.9
  59.0 4.4 %collective-permute-start.4 = (f32[4,3,4,1,128]{4,3,2,1,0:T(1,128)S(1)}, f32[4,3,4,1,128]{4,3,2,1,0:T(1,128)S(1)}, u32[]{:S(2)}, u32[]{:S(2)}) collective-permute-start(f32[4,3,4,1,128]{4,3,2,1,0:T(1,128)S(1)} %get-tuple-element.663), channel_id=1, source_target_pairs={{0,1},{1,0},{2,3},{3,2},{4,5},{5,4},{6,7},{7,6},{8,9},{9,8},{10,11... | collective-permute-start | bytes 73736 | tf_op jit(solution)/shard_map/ppermute | solution.py:19
  59.8 3.8 collective-permute-start.5
  61.2 4.0 %collective-permute-start.10 = (f32[6,3,4,1,128]{4,3,2,0,1:T(1,128)S(1)}, f32[6,3,4,1,128]{4,3,2,0,1:T(1,128)S(1)}, u32[]{:S(2)}, u32[]{:S(2)}) collective-permute-start(f32[6,3,4,1,128]{4,3,2,0,1:T(1,128)S(1)} %get-tuple-element.661), channel_id=1, source_target_pairs={{0,1},{1,0},{2,3},{3,2},{4,5},{5,4},{6,7},{7,6},{8,9},{9,8},{10,11... | collective-permute-start | bytes 110600 | tf_op jit(solution)/shard_map/ppermute | solution.py:19
  62.0 4.0 collective-permute-start.11
  66.1 134.4 %copy-start.3 = (f32[6,1,2,2,128]{4,3,2,1,0:T(2,128)S(1)}, f32[6,1,2,2,128]{4,3,2,1,0:T(2,128)}, u32[]{:S(2)}) copy-start(f32[6,1,2,2,128]{4,3,2,1,0:T(2,128)} %param.14) | copy-start | bytes 36868
  200.5 3.2 collective-permute-start.12
  200.6 3.1 collective-permute-start.13
  203.8 4.9 %collective-permute-start.14 = (f32[6,3,1,2,128]{4,3,2,1,0:T(2,128)S(1)}, f32[6,3,1,2,128]{4,3,2,1,0:T(2,128)S(1)}, u32[]{:S(2)}, u32[]{:S(2)}) collective-permute-start(f32[6,3,1,2,128]{4,3,2,1,0:T(2,128)S(1)} %get-tuple-element.665), channel_id=1, source_target_pairs={{0,2},{2,4},{4,6},{6,0},{1,3},{3,5},{5,7},{7,1},{8,10},{10,12},{12... | collective-permute-start | bytes 55304 | tf_op jit(solution)/shard_map/ppermute | solution.py:19
  206.1 5.1 %collective-permute-start.15 = (f32[6,3,1,2,128]{4,3,2,1,0:T(2,128)S(1)}, f32[6,3,1,2,128]{4,3,2,1,0:T(2,128)S(1)}, u32[]{:S(2)}, u32[]{:S(2)}) collective-permute-start(f32[6,3,1,2,128]{4,3,2,1,0:T(2,128)S(1)} %get-tuple-element.666), channel_id=1, source_target_pairs={{2,0},{4,2},{6,4},{0,6},{3,1},{5,3},{7,5},{1,7},{10,8},{12,10},{14... | collective-permute-start | bytes 55304 | tf_op jit(solution)/shard_map/ppermute | solution.py:21
  211.3 4.2 %collective-permute-start.16 = (f32[6,3,4,1,128]{4,3,2,1,0:T(1,128)S(1)}, f32[6,3,4,1,128]{4,3,2,1,0:T(1,128)S(1)}, u32[]{:S(2)}, u32[]{:S(2)}) collective-permute-start(f32[6,3,4,1,128]{4,3,2,1,0:T(1,128)S(1)} %get-tuple-element.659), channel_id=1, source_target_pairs={{0,1},{1,0},{2,3},{3,2},{4,5},{5,4},{6,7},{7,6},{8,9},{9,8},{10,11... | collective-permute-start | bytes 110600 | tf_op jit(solution)/shard_map/ppermute | solution.py:19
  212.8 4.0 collective-permute-start.17
where the time goes:
time: 398 us; the launch traced here: 396 us
  other arithmetic  220 us (55%)
  blocking collectives  83 us (21%)
  local copies, waits for them, and re-layouts  45.7 us (11%)
  starting transfers between devices  19.3 us (5%)
  waiting for transfers between devices  12.7 us (3%)
  loops' own time  10.9 us (3%)
    reduce_sum x108, other arithmetic, pair_field(): jnp.sum(radial * project * displace[axis_num] - direct * parts[axis_num],...  102 us
    slice x27, other arithmetic, pair_field(): moment[3 * which_set + axis_num][:, None, :]  52 us
    add x27, other arithmetic, pair_field(): offset_vec[axis_num] + source[axis_num][:, None, :]  51.6 us
    psum x1, blocking collectives, on_device(): lax.psum((jnp.sum(update * update), jnp.sum(induced * induced)), ('gx', '...  41.8 us
    psum x1, blocking collectives, global_gram(): return lax.psum(local_gram, ('gx', 'gy', 'gz'))  41.2 us
    slice x54, local copies, waits for them, and re-layouts, pair_field(): offset_vec[axis_num] + source[axis_num][:, None, :]  36 us
    ppermute x9, starting transfers between devices, with_halo(): lax.ppermute(head, axis, [((i + 1) % count, i) for i in range(count)])  10.9 us
    another operation x2, loops' own time, slab_field(): lax.fori_loop(0, 27, offset_step, jnp.zeros((rows, width_y * width_z, slo...  10.9 us
  transfers between devices with their start and end apart: 18, of which 11 were waited for; matrix products, arithmetic and copies ran while one was open for 0% of the time, Pallas kernels for 0%

commit v1 on v0

--- a/solution.py
+++ b/solution.py
@@ -108,7 +108,7 @@
 
 
 def global_gram(local_gram):
-    return lax.psum(local_gram, ("gx", "gy", "gz"))
+    return jnp.sum(lax.all_gather(local_gram, ("gx", "gy", "gz")), axis=0)
 
 
 def fit_coefficients(gram_matrix):

time: 398 us -> 425 us (1.068)
  blocking collectives: 83 us -> 108 us
    all_gather x0 -> x1, blocking collectives: none -> 65.1 us  [global_gram(): return jnp.sum(lax.all_gather(local_gram, ('gx', 'gy', 'gz')), axis=0)]
    psum x1 -> x0, blocking collectives: 41.2 us -> none  [global_gram(): return lax.psum(local_gram, ('gx', 'gy', 'gz'))]
    ppermute x9, starting transfers between devices: 10.9 us -> 17.6 us  [with_halo(): lax.ppermute(head, axis, [((i + 1) % count, i) for i in range(count)])]
  transfers between devices with their start and end apart: 18 -> 18, of which waited for: 11 -> 9; matrix products, arithmetic and copies ran while one was open for 0% -> 0% of each run, Pallas kernels for 0% -> 0%
where the time goes in v1:
time: 425 us; the launch traced here: 423 us
  other arithmetic  220 us (52%)
  blocking collectives  108 us (25%)
  local copies, waits for them, and re-layouts  45.4 us (11%)
  starting transfers between devices  22.8 us (5%)
  waiting for transfers between devices  12.1 us (3%)
  loops' own time  10.9 us (3%)
    reduce_sum x108, other arithmetic, pair_field(): jnp.sum(radial * project * displace[axis_num] - direct * parts[axis_num],...  102 us
    all_gather x1, blocking collectives, global_gram(): return jnp.sum(lax.all_gather(local_gram, ('gx', 'gy', 'gz')), axis=0)  65.1 us
    slice x27, other arithmetic, pair_field(): moment[3 * which_set + axis_num][:, None, :]  52 us
    add x27, other arithmetic, pair_field(): offset_vec[axis_num] + source[axis_num][:, None, :]  51.6 us
    psum x1, blocking collectives, on_device(): lax.psum((jnp.sum(update * update), jnp.sum(induced * induced)), ('gx', '...  42.7 us
    slice x54, local copies, waits for them, and re-layouts, pair_field(): offset_vec[axis_num] + source[axis_num][:, None, :]  36 us
    ppermute x9, starting transfers between devices, with_halo(): lax.ppermute(head, axis, [((i + 1) % count, i) for i in range(count)])  17.6 us
    another operation x2, loops' own time, slab_field(): lax.fori_loop(0, 27, offset_step, jnp.zeros((rows, width_y * width_z, slo...  10.9 us
  transfers between devices with their start and end apart: 18, of which 9 were waited for; matrix products, arithmetic and copies ran while one was open for 0% of the time, Pallas kernels for 0%

profile of v1, /device:TPU:12, one launch (start us, length us, event | category | flops | bytes accessed | tf_op | source)
XLA Modules:
  0.0 423.3 jit_solution(191777927832230305)
XLA Ops:
  2.6 65.1 %all-gather.1 = f32[32,6,6]{2,1,0:T(8,128)S(1)} all-gather(f32[1,6,6]{2,1,0:T(8,128)S(1)} %convolution_bitcast_fusion), channel_id=2, replica_groups=mesh['gx'=4,'gy'=4,'gz'=2] {'gx','gy','gz'}, dimensions={0}, use_global_device_ids=true | all-gather | bytes 4752 | tf_op jit(solution)/shard_map/all_gather | solution.py:111
  77.5 3.3 collective-permute-start.3
  81.0 3.8 collective-permute-start.9
  85.0 2.0 collective-permute-start.5
  87.2 1.9 collective-permute-start.11
  91.6 134.4 %while.38 = (s32[]{:T(128)}, f32[6,4,128]{2,1,0:T(4,128)S(1)}, f32[4,3,4,4,128]{4,3,2,1,0:T(4,128)S(1)}, f32[4,4,128]{2,1,0:T(4,128)S(1)}, s32[2,2,27]{1,0,2:T(2...) while((s32[]{:T(128)}, f32[6,4,128]{2,1,0:T(4,128)S(1)}, ...), condition=%wide.region_11.12_spmd.clone, body=%wide.region_4.11_spmd.clone.sunk | while | flops 6200888 | bytes 287493 | solution.py:95
  102.5 1.9 dynamic-slice_add_fusion.4
  107.5 1.9 dynamic-slice_add_fusion.4
  117.4 1.9 dynamic-slice_add_fusion.4
  122.4 1.9 dynamic-slice_add_fusion.4
  127.4 1.9 dynamic-slice_add_fusion.4
  137.3 1.9 dynamic-slice_add_fusion.4
  142.3 1.9 dynamic-slice_add_fusion.4
  147.3 1.9 dynamic-slice_add_fusion.4
  157.2 1.9 dynamic-slice_add_fusion.4
  162.2 1.9 dynamic-slice_add_fusion.4
  229.3 3.0 collective-permute-start.14
  234.9 2.6 collective-permute-done.15
  239.6 1.9 collective-permute-done.16
  243.3 133.6 %while.39 = (s32[]{:T(128)}, f32[6,4,128]{2,1,0:T(4,128)S(1)}, f32[4,3,4,4,128]{4,3,2,1,0:T(4,128)S(1)}, f32[4,4,128]{2,1,0:T(4,128)S(1)}, s32[2,2,27]{1,0,2:T(2...) while((s32[]{:T(128)}, f32[6,4,128]{2,1,0:T(4,128)S(1)}, ...), condition=%wide.region_19.20_spmd.clone, body=%wide.region_12.19_spmd.clone.sunk | while | flops 6200890 | bytes 262953 | solution.py:95
  244.1 1.9 constant_dynamic-slice_fusion.14
  249.1 1.9 constant_dynamic-slice_fusion.14
  254.0 1.9 constant_dynamic-slice_fusion.14
  259.0 1.9 constant_dynamic-slice_fusion.14
  263.9 1.9 constant_dynamic-slice_fusion.14
  268.8 1.9 constant_dynamic-slice_fusion.14
  273.8 1.9 constant_dynamic-slice_fusion.14
  278.7 1.9 constant_dynamic-slice_fusion.14
  283.7 1.9 constant_dynamic-slice_fusion.14
  288.6 1.9 constant_dynamic-slice_fusion.14
  293.6 1.9 constant_dynamic-slice_fusion.14
  298.5 1.9 constant_dynamic-slice_fusion.14
  303.5 1.9 constant_dynamic-slice_fusion.14
  308.4 1.9 constant_dynamic-slice_fusion.14
  313.4 1.9 constant_dynamic-slice_fusion.14
  318.3 1.9 constant_dynamic-slice_fusion.14
  323.3 1.9 constant_dynamic-slice_fusion.14
  328.2 1.9 constant_dynamic-slice_fusion.14
  333.2 1.9 constant_dynamic-slice_fusion.14
  338.1 1.9 constant_dynamic-slice_fusion.14
  343.1 1.9 constant_dynamic-slice_fusion.14
  348.0 1.9 constant_dynamic-slice_fusion.14
  353.0 1.9 constant_dynamic-slice_fusion.14
  357.9 1.9 constant_dynamic-slice_fusion.14
  362.9 1.9 constant_dynamic-slice_fusion.14
  367.8 1.9 constant_dynamic-slice_fusion.14
  372.8 1.9 constant_dynamic-slice_fusion.14
  378.2 42.7 %all-reduce = (f32[]{:T(128)}, f32[]{:T(128)}) all-reduce(f32[]{:T(128)} %get-tuple-element.613, f32[]{:T(128)} %get-tuple-element.612), channel_id=1, replica_groups=mesh['gx'=4,'gy'=4,'gz'=2] {'gx','gy','gz'}, use_global_device_ids=true, to_apply=%region_21.22 | all-reduce | flops 2 | bytes 16 | tf_op jit(solution)/shard_map/psum | solution.py:140
  (1237 shorter events, 211.0 us)
Async XLA Ops:
  1.3 1.0 copy-start
  72.2 2.1 copy-start.1
  72.4 1.8 copy-start.2
  72.4 8.5 %collective-permute-start.6 = (f32[6,1,2,2,128]{4,3,2,0,1:T(2,128)S(1)}, f32[6,1,2,2,128]{4,3,2,0,1:T(2,128)S(1)}, u32[]{:S(2)}, u32[]{:S(2)}) collective-permute-start(f32[6,1,2,2,128]{4,3,2,0,1:T(2,128)S(1)} %bitcast.226), channel_id=1, source_target_pairs={{0,8},{8,16},{16,24},{24,0},{1,9},{9,17},{17,25},{25,1},{2,10},{10... | collective-permute-start | bytes 36872 | tf_op jit(solution)/shard_map/ppermute | solution.py:19
  72.5 8.4 %collective-permute-start.7 = (f32[6,1,2,2,128]{4,3,2,0,1:T(2,128)S(1)}, f32[6,1,2,2,128]{4,3,2,0,1:T(2,128)S(1)}, u32[]{:S(2)}, u32[]{:S(2)}) collective-permute-start(f32[6,1,2,2,128]{4,3,2,0,1:T(2,128)S(1)} %bitcast.227), channel_id=1, source_target_pairs={{8,0},{16,8},{24,16},{0,24},{9,1},{17,9},{25,17},{1,25},{10,2},{18... | collective-permute-start | bytes 36872 | tf_op jit(solution)/shard_map/ppermute | solution.py:21
  74.2 1.8 copy-start.4
  74.2 3.2 collective-permute-start
  74.3 3.1 collective-permute-start.1
  76.0 0.7 copy-start.5
  77.5 7.3 %collective-permute-start.2 = (f32[4,3,1,2,128]{4,3,2,1,0:T(2,128)S(1)}, f32[4,3,1,2,128]{4,3,2,1,0:T(2,128)S(1)}, u32[]{:S(2)}, u32[]{:S(2)}) collective-permute-start(f32[4,3,1,2,128]{4,3,2,1,0:T(2,128)S(1)} %get-tuple-element.693), channel_id=1, source_target_pairs={{0,2},{2,4},{4,6},{6,0},{1,3},{3,5},{5,7},{7,1},{8,10},{10,12},{12... | collective-permute-start | bytes 36872 | tf_op jit(solution)/shard_map/ppermute | solution.py:19
  77.5 7.3 %collective-permute-start.3 = (f32[4,3,1,2,128]{4,3,2,1,0:T(2,128)S(1)}, f32[4,3,1,2,128]{4,3,2,1,0:T(2,128)S(1)}, u32[]{:S(2)}, u32[]{:S(2)}) collective-permute-start(f32[4,3,1,2,128]{4,3,2,1,0:T(2,128)S(1)} %get-tuple-element.694), channel_id=1, source_target_pairs={{2,0},{4,2},{6,4},{0,6},{3,1},{5,3},{7,5},{1,7},{10,8},{12,10},{14... | collective-permute-start | bytes 36872 | tf_op jit(solution)/shard_map/ppermute | solution.py:21
  80.9 6.1 %collective-permute-start.8 = (f32[6,3,1,2,128]{4,3,2,0,1:T(2,128)S(1)}, f32[6,3,1,2,128]{4,3,2,0,1:T(2,128)S(1)}, u32[]{:S(2)}, u32[]{:S(2)}) collective-permute-start(f32[6,3,1,2,128]{4,3,2,0,1:T(2,128)S(1)} %get-tuple-element.691), channel_id=1, source_target_pairs={{0,2},{2,4},{4,6},{6,0},{1,3},{3,5},{5,7},{7,1},{8,10},{10,12},{12... | collective-permute-start | bytes 55304 | tf_op jit(solution)/shard_map/ppermute | solution.py:19
  81.0 6.0 %collective-permute-start.9 = (f32[6,3,1,2,128]{4,3,2,0,1:T(2,128)S(1)}, f32[6,3,1,2,128]{4,3,2,0,1:T(2,128)S(1)}, u32[]{:S(2)}, u32[]{:S(2)}) collective-permute-start(f32[6,3,1,2,128]{4,3,2,0,1:T(2,128)S(1)} %get-tuple-element.692), channel_id=1, source_target_pairs={{2,0},{4,2},{6,4},{0,6},{3,1},{5,3},{7,5},{1,7},{10,8},{12,10},{14... | collective-permute-start | bytes 55304 | tf_op jit(solution)/shard_map/ppermute | solution.py:21
  84.9 4.3 %collective-permute-start.4 = (f32[4,3,4,1,128]{4,3,2,1,0:T(1,128)S(1)}, f32[4,3,4,1,128]{4,3,2,1,0:T(1,128)S(1)}, u32[]{:S(2)}, u32[]{:S(2)}) collective-permute-start(f32[4,3,4,1,128]{4,3,2,1,0:T(1,128)S(1)} %get-tuple-element.687), channel_id=1, source_target_pairs={{0,1},{1,0},{2,3},{3,2},{4,5},{5,4},{6,7},{7,6},{8,9},{9,8},{10,11... | collective-permute-start | bytes 73736 | tf_op jit(solution)/shard_map/ppermute | solution.py:19
  85.0 4.4 %collective-permute-start.5 = (f32[4,3,4,1,128]{4,3,2,1,0:T(1,128)S(1)}, f32[4,3,4,1,128]{4,3,2,1,0:T(1,128)S(1)}, u32[]{:S(2)}, u32[]{:S(2)}) collective-permute-start(f32[4,3,4,1,128]{4,3,2,1,0:T(1,128)S(1)} %get-tuple-element.688), channel_id=1, source_target_pairs={{1,0},{0,1},{3,2},{2,3},{5,4},{4,5},{7,6},{6,7},{9,8},{8,9},{11,10... | collective-permute-start | bytes 73736 | tf_op jit(solution)/shard_map/ppermute | solution.py:21
  87.1 4.0 collective-permute-start.10
  87.2 4.3 %collective-permute-start.11 = (f32[6,3,4,1,128]{4,3,2,0,1:T(1,128)S(1)}, f32[6,3,4,1,128]{4,3,2,0,1:T(1,128)S(1)}, u32[]{:S(2)}, u32[]{:S(2)}) collective-permute-start(f32[6,3,4,1,128]{4,3,2,0,1:T(1,128)S(1)} %get-tuple-element.686), channel_id=1, source_target_pairs={{1,0},{0,1},{3,2},{2,3},{5,4},{4,5},{7,6},{6,7},{9,8},{8,9},{11,10... | collective-permute-start | bytes 110600 | tf_op jit(solution)/shard_map/ppermute | solution.py:21
  91.6 134.4 %copy-start.3 = (f32[6,1,2,2,128]{4,3,2,1,0:T(2,128)S(1)}, f32[6,1,2,2,128]{4,3,2,1,0:T(2,128)}, u32[]{:S(2)}) copy-start(f32[6,1,2,2,128]{4,3,2,1,0:T(2,128)} %param.14) | copy-start | bytes 36868
  226.1 3.2 collective-permute-start.12
  226.1 3.1 collective-permute-start.13
  229.3 5.5 %collective-permute-start.14 = (f32[6,3,1,2,128]{4,3,2,1,0:T(2,128)S(1)}, f32[6,3,1,2,128]{4,3,2,1,0:T(2,128)S(1)}, u32[]{:S(2)}, u32[]{:S(2)}) collective-permute-start(f32[6,3,1,2,128]{4,3,2,1,0:T(2,128)S(1)} %get-tuple-element.689), channel_id=1, source_target_pairs={{0,2},{2,4},{4,6},{6,0},{1,3},{3,5},{5,7},{7,1},{8,10},{10,12},{12... | collective-permute-start | bytes 55304 | tf_op jit(solution)/shard_map/ppermute | solution.py:19
  232.3 5.1 %collective-permute-start.15 = (f32[6,3,1,2,128]{4,3,2,1,0:T(2,128)S(1)}, f32[6,3,1,2,128]{4,3,2,1,0:T(2,128)S(1)}, u32[]{:S(2)}, u32[]{:S(2)}) collective-permute-start(f32[6,3,1,2,128]{4,3,2,1,0:T(2,128)S(1)} %get-tuple-element.690), channel_id=1, source_target_pairs={{2,0},{4,2},{6,4},{0,6},{3,1},{5,3},{7,5},{1,7},{10,8},{12,10},{14... | collective-permute-start | bytes 55304 | tf_op jit(solution)/shard_map/ppermute | solution.py:21
  237.5 4.0 collective-permute-start.16
  239.2 4.0 collective-permute-start.17
